TPU v7x, 32 devices: a whole 2x2x4 slice. The times are simulated.
32 devices in a mesh: rows: 4 (over y, core), cols: 8 (over z, x), hub: 1.
Axes of the slice: x: 2, y: 2, z: 4, core: 2. Of those that a mesh axis runs over, the one named last changes fastest.
Arguments:
- light_bits: int32 [96, 3072], P('rows', 'cols'), may hold values from -2147483648 to 2147483647, as said below
- hub_bits: int32 [4, 3072], P('hub', 'cols'), may hold values from -2147483648 to 2147483647, as said below
- hub_ids: int32 [128], replicated, may hold values from 0 to 3071, as said below
Outputs:
- clustering: float32 [3072], P(('rows', 'cols'))
Inputs may be any that keep to these rules, and one draw needn't show every extreme that they name: Every word holds 32 bits; the matrix of light_bits is symmetric with a zero diagonal. `hub_bits`: every word holds 32 bits. `hub_ids`: 128 distinct vertex numbers.
All inputs are finite; a program needn't handle non-finite values.
Results may differ from a plain program's by a relative error of at most 0.0003.
Values sent between devices are 32-bit elements; how exact they have to be, the bound alone decides.
A program may use at most 128 MiB of HBM per device.

v0:
```python
import jax
import jax.numpy as jnp
from jax import lax
from jax.sharding import PartitionSpec as P


def unpack(packed):
    shifts = jnp.arange(32, dtype=jnp.int32)
    bit_grid = jnp.bitwise_and(jnp.right_shift(packed[:, None, :], shifts[None, :, None]), 1)
    return bit_grid.reshape(packed.shape[0] * 32, packed.shape[1]).astype(jnp.bfloat16)


def light_flags(anchor, amount, hub_ids):
    vertex_ids = anchor + lax.iota(jnp.int32, amount)
    is_hub = jnp.any(vertex_ids[:, None] == hub_ids[None, :], axis=1)
    return jnp.where(is_hub, 0.0, 1.0).astype(jnp.bfloat16)


def body(light_bits, hub_bits, hub_ids):
    row_idx = lax.axis_index("rows")
    col_idx = lax.axis_index("cols")
    group_idx = lax.axis_index("hub")
    groups = lax.axis_size("hub")
    col_devices = lax.axis_size("cols")
    block_words = light_bits.shape[0]
    block_rows = 32 * block_words
    block_cols = light_bits.shape[1]
    row_base = row_idx * block_rows
    col_base = col_idx * block_cols
    row_keep = light_flags(row_base, block_rows, hub_ids)
    col_keep = light_flags(col_base, block_cols, hub_ids)
    adjacent = unpack(light_bits) * row_keep[:, None] * col_keep[None, :]
    row_start = 0
    part_cols = block_cols // groups
    col_start = group_idx * part_cols
    column_words = lax.dynamic_slice_in_dim(light_bits, col_start, part_cols, 1)
    row_packed = lax.all_gather(light_bits, "cols", axis=1, tiled=True)
    section = lax.all_gather(column_words, "rows", axis=0, tiled=True)
    vertex_start = 32 * jnp.int32(0)
    section_rows = 32 * section.shape[0]
    keep_mid = light_flags(vertex_start, section_rows, hub_ids)
    column_bits = unpack(section) * keep_mid[:, None]
    row_slice = unpack(row_packed)
    two_paths = jnp.dot(row_slice, column_bits, preferred_element_type=jnp.float32)
    two_paths = two_paths * row_keep.astype(jnp.float32)[:, None]
    own_part = lax.dynamic_slice(adjacent, (row_start, col_start), (block_rows, part_cols)).astype(
        jnp.float32
    )
    light_tri = 0.5 * jnp.sum(own_part * two_paths, axis=1)
    light_deg = jnp.sum(own_part, axis=1)
    tri_vec = light_tri
    deg_vec = light_deg
    group_hubs = 32 * hub_bits.shape[0]
    hub_cols = unpack(hub_bits) * col_keep[None, :]
    hub_whole = lax.all_gather(hub_bits, "cols", axis=1, tiled=True)
    hub_here = (
        unpack(lax.dynamic_slice_in_dim(hub_whole, row_base, block_rows, 1)) * row_keep[None, :]
    )
    reach_hub = lax.dot_general(
        hub_cols, adjacent, (((1,), (1,)), ((), ())), preferred_element_type=jnp.float32
    )
    intersect = hub_here.astype(jnp.float32) * reach_hub
    first_col = (col_idx == 0).astype(jnp.float32)
    first_row = (row_idx == 0).astype(jnp.float32)
    tri_vec = tri_vec + jnp.sum(intersect, axis=0)
    deg_vec = deg_vec + first_col * jnp.sum(hub_here.astype(jnp.float32), axis=0)
    hub_tri = 0.5 * jnp.sum(intersect, axis=1)
    hub_deg = first_row * jnp.sum(hub_cols.astype(jnp.float32), axis=1)
    all_hubs = hub_ids.shape[0]
    hub_tri_full = lax.dynamic_update_slice_in_dim(
        jnp.zeros((all_hubs,), jnp.float32), hub_tri, group_idx * group_hubs, 0
    )
    hub_deg_full = lax.dynamic_update_slice_in_dim(
        jnp.zeros((all_hubs,), jnp.float32), hub_deg, group_idx * group_hubs, 0
    )
    hub_tri_full, hub_deg_full = lax.psum((hub_tri_full, hub_deg_full), ("rows", "cols", "hub"))
    per_device = block_rows // col_devices
    tri_whole, deg_whole = lax.psum((tri_vec, deg_vec), ("cols", "hub"))
    tri_mine = lax.dynamic_slice_in_dim(tri_whole, col_idx * per_device, per_device, 0)
    deg_mine = lax.dynamic_slice_in_dim(deg_whole, col_idx * per_device, per_device, 0)
    vertex_ids = row_base + col_idx * per_device + lax.iota(jnp.int32, per_device)
    owners = (vertex_ids[:, None] == hub_ids[None, :]).astype(jnp.float32)
    tri_mine = tri_mine + jnp.sum(owners * hub_tri_full[None, :], axis=1)
    deg_mine = deg_mine + jnp.sum(owners * hub_deg_full[None, :], axis=1)
    return tri_mine / (1.0 + deg_mine)


def solution(mesh):
    return jax.shard_map(
        body,
        mesh=mesh,
        in_specs=(P("rows", "cols"), P("hub", "cols"), P()),
        out_specs=P(("rows", "cols")),
        check_vma=False,
    )
```

profile of v0, /device:TPU:0, one launch (start us, length us, event | category | flops | bytes accessed | tf_op | source)
XLA Modules:
  0.0 142.8 jit_solution(10749890620294315225)
XLA Ops:
  0.0 0.0 copy-start
  0.0 0.9 compare_reduce_fusion.1
  0.9 0.8 convert_reduce_fusion.2
  1.7 0.1 mul.197
  1.8 0.1 shift_right_arithmetic.136
  1.9 1.1 fusion.1
  3.1 1.0 compare_reduce_fusion
  4.0 0.1 convert_element_type.132
  4.1 1.2 convert_reduce_fusion
  5.3 0.1 reduce_sum.79
  5.4 0.1 shift_right_arithmetic.124
  5.5 0.1 convert_element_type.126
  5.6 32.8 %all_gather.11 = s32[4,3072]{1,0:T(4,128)S(1)} all-gather(s32[4,384]{1,0:T(4,128)} %param.4), channel_id=1, replica_groups=mesh['rows'=4,'cols'=8,'hub'=1] {'cols'}, dimensions={1}, use_global_device_ids=true | all-gather | bytes 55296 | tf_op jit(solution)/shard_map/all_gather | solution.py:55
  38.4 0.1 convert_reduce_fusion.1
  38.5 0.0 copy-start.1
  38.5 0.7 fusion.12
  39.2 5.7 %all_gather.10 = s32[96,384]{1,0:T(8,128)S(1)} all-gather(s32[24,384]{1,0:T(8,128)} %param.3), channel_id=1, replica_groups=mesh['rows'=4,'cols'=8,'hub'=1] {'rows'}, dimensions={0}, use_global_device_ids=true | all-gather | bytes 184320 | tf_op jit(solution)/shard_map/all_gather | solution.py:38
  44.9 0.1 fusion.11
  45.0 31.0 %all_gather.9 = s32[24,3072]{1,0:T(8,128)S(1)} all-gather(s32[24,384]{1,0:T(8,128)} %param.3), channel_id=1, replica_groups=mesh['rows'=4,'cols'=8,'hub'=1] {'cols'}, dimensions={1}, use_global_device_ids=true | all-gather | bytes 331776 | tf_op jit(solution)/shard_map/all_gather | solution.py:37
  76.0 0.0 copy-done
  76.0 0.3 fusion.7
  76.3 0.4 fusion.16
  76.7 39.5 %all-reduce = (f32[128]{0:T(128)S(1)}, f32[128]{0:T(128)S(1)}) all-reduce(f32[128]{0:T(128)S(1)} %broadcast_multiply_fusion.1, f32[128]{0:T(128)S(1)} %mul.197), channel_id=1, replica_groups=mesh['rows'=4,'cols'=8,'hub'=1] {'rows','cols','hub'}, use_global_device_ids=true, to_apply=%region_7.8 | all-reduce | flops 256 | bytes 2048 | tf_op jit(solution)/shard_map/psum | solution.py:76
  116.3 0.0 copy-done.1
  116.3 0.2 fusion.13
  116.4 0.1 shift_right_arithmetic.121
  116.5 0.4 copy.6
  116.9 0.9 fusion
  117.8 1.4 and_convert_fusion
  119.2 2.3 %fusion.3 = f32[768]{0:T(1024)S(1)} fusion(bf16[768,3072]{1,0:T(8,128)(2,1)S(1)} %bitcast.17, bf16[3072,384]{1,0:T(8,128)(2,1)S(1)} %bitcast.19, s32[768,384]{0,1:T(8,128)S(1)} %copy.6, f32[768]{0:T(1024)S(1)} %get-tuple-element.13, s32[768]{0:T(1024)S(1)} %shift_right_arithmetic.124, bf16[384]{0:T(512)(128)(2,1)S(1)} %select_convert_fusion.2, ...), kind=kOutput, calls=%fused_computation.7 | convolution fusion | flops 1815477504 | bytes 8269056 | tf_op jit(solution)/shard_map/dot_general | solution.py:44
  121.6 20.6 %all-reduce.1 = (f32[768]{0:T(1024)S(1)}, f32[768]{0:T(1024)S(1)}) all-reduce(f32[768]{0:T(1024)S(1)} %multiply_add_fusion, f32[768]{0:T(1024)S(1)} %multiply_add_fusion.1), channel_id=1, replica_groups=mesh['rows'=4,'cols'=8,'hub'=1] {'cols','hub'}, use_global_device_ids=true, to_apply=%region_11.12 | all-reduce | flops 1536 | bytes 12288 | tf_op jit(solution)/shard_map/psum | solution.py:78
  142.2 0.6 add_divide_fusion
  (13 shorter events, 0.1 us)
Async XLA Ops:
  0.0 76.0 %copy-start = (s32[24,384]{1,0:T(8,128)S(1)}, s32[24,384]{1,0:T(8,128)}, u32[]{:S(2)}) copy-start(s32[24,384]{1,0:T(8,128)} %param.3) | copy-start | bytes 110596
  38.5 77.8 %copy-start.1 = (s32[128]{0:T(128)S(1)}, s32[128]{0:T(128)}, u32[]{:S(2)}) copy-start(s32[128]{0:T(128)} %param.5) | copy-start | bytes 1540
where the time goes:
time: 143 us
  blocking collectives  130 us (91%)
  other arithmetic  9.4 us (7%)
  matrix products  2.72 us (2%)
    psum x1, blocking collectives, body(): lax.psum((hub_tri_full, hub_deg_full), ('rows', 'cols', 'hub'))  39.5 us
    all_gather x1, blocking collectives, body(): hub_whole = lax.all_gather(hub_bits, 'cols', axis=1, tiled=True)  32.8 us
    all_gather x1, blocking collectives, body(): row_packed = lax.all_gather(light_bits, 'cols', axis=1, tiled=True)  31 us
    psum x1, blocking collectives, body(): tri_whole, deg_whole = lax.psum((tri_vec, deg_vec), ('cols', 'hub'))  20.6 us
    all_gather x1, blocking collectives, body(): section = lax.all_gather(column_words, 'rows', axis=0, tiled=True)  5.67 us
    reduce_or x3, other arithmetic, light_flags(): is_hub = jnp.any(vertex_ids[:, None] == hub_ids[None, :], axis=1)  2.99 us

commit v1 on v0

v1 whole, which is shorter than its diff:
```python
import functools

import jax
import jax.numpy as jnp
from jax import lax
from jax.experimental import pallas as pl
from jax.experimental.pallas import tpu as pltpu
from jax.sharding import PartitionSpec as P

LANES = 128
MESH = pl.DeviceIdType.MESH


def spread(row, value, other=0.0):
    masks = jnp.left_shift(jnp.int32(1), lax.broadcasted_iota(jnp.int32, (32, row.shape[1]), 0))
    return jnp.where((jnp.broadcast_to(row, masks.shape) & masks) != 0, value, other)


def kernel(
    R, C, G,
    light_hbm, hub_hbm, ids_ref, out_ref,
    rowbuf, colbuf, hubbuf, keep, hubcol, abuf, bbuf, acc, wsum, outbox, inbox,
    local_sem, row_send, row_recv, col_send, col_recv, hub_send, hub_recv, msg_send, msg_recv,
):
    r, c, g = lax.axis_index("rows"), lax.axis_index("cols"), lax.axis_index("hub")
    _, bw, bc = rowbuf.shape
    hw = hubbuf.shape[1]
    pc = bc // G
    q = C // R
    rows = 32 * bw
    nh = 32 * hw * G
    per = rows // C
    me = g * C + c

    own = [
        pltpu.make_async_copy(light_hbm, rowbuf.at[c], local_sem.at[0]),
        pltpu.make_async_copy(hub_hbm, hubbuf.at[me], local_sem.at[1]),
        pltpu.make_async_copy(light_hbm, colbuf.at[r], local_sem.at[2]),
    ]
    for copy in own:
        copy.start()

    def group_peer(d):
        slot = lax.rem(me + d, G * C)
        return slot, (r, lax.rem(slot, C), slot // C)

    def col_peer(d):
        slot = lax.rem(r + d, R)
        return slot, (slot, c, g)

    barrier = pltpu.get_barrier_semaphore()
    for d in range(1, G * C):
        pl.semaphore_signal(barrier, inc=1, device_id=group_peer(d)[1], device_id_type=MESH)
    for d in range(1, R):
        pl.semaphore_signal(barrier, inc=1, device_id=col_peer(d)[1], device_id_type=MESH)

    for copy in own:
        copy.wait()
    pl.semaphore_wait(barrier, G * C - 1 + R - 1)

    sends = []
    for d in range(1, C):
        to = lax.rem(c + d, C)
        sends.append(pltpu.make_async_remote_copy(
            src_ref=rowbuf.at[c], dst_ref=rowbuf.at[c], send_sem=row_send.at[d], recv_sem=row_recv.at[c],
            device_id=(r, to, g), device_id_type=MESH))
    for d in range(1, R):
        sends.append(pltpu.make_async_remote_copy(
            src_ref=colbuf.at[r], dst_ref=colbuf.at[r], send_sem=col_send.at[d], recv_sem=col_recv.at[r],
            device_id=col_peer(d)[1], device_id_type=MESH))
    for d in range(1, G * C):
        sends.append(pltpu.make_async_remote_copy(
            src_ref=hubbuf.at[me], dst_ref=hubbuf.at[me], send_sem=hub_send.at[d], recv_sem=hub_recv.at[me],
            device_id=group_peer(d)[1], device_id_type=MESH))
    for copy in sends:
        copy.start()

    for h in range(nh // LANES):
        hubcol[h * LANES:(h + 1) * LANES, :] = jnp.transpose(
            jnp.broadcast_to(ids_ref[h:h + 1, :], (LANES, LANES)))

    def hub_hits(base):
        return hubcol[...] == base + lax.broadcasted_iota(jnp.int32, (nh, LANES), 1)

    def light_lanes(t, carry):
        hit = jnp.max(jnp.where(hub_hits(t * LANES), 1, 0), axis=0, keepdims=True)
        keep[pl.ds(t, 1), :] = hit - 1
        return carry

    tiles = bc // LANES
    lax.fori_loop(0, C * tiles, light_lanes, 0)

    def keep_of(block):
        return jnp.concatenate([keep[pl.ds(block * tiles + t, 1), :] for t in range(tiles)], axis=1)

    bbuf[:, pc:] = jnp.full((bbuf.shape[0], LANES), 1.0, jnp.bfloat16)
    part = pl.ds(pl.multiple_of(g * pc, LANES), pc)
    acc[...] = jnp.zeros_like(acc)

    def step(s, carry):
        off = (s + 1) // 2 if isinstance(s, int) and s % 2 else None
        if isinstance(s, int):
            off = (s + 1) // 2 if s % 2 else R - s // 2
        else:
            off = lax.select(lax.rem(s, 2) == 1, (s + 1) // 2, R - s // 2)
        rk = lax.rem(c // q + off, R)

        @pl.when(rk != r)
        def _():
            pltpu.make_async_copy(colbuf.at[rk], colbuf.at[rk], col_recv.at[rk]).wait()

        for w in range(bw):
            bbuf[32 * w:32 * w + 32, :pc] = spread(colbuf[rk, w:w + 1, part], 1.0).astype(jnp.bfloat16)
        for k in range(q):
            ck = rk * q + k

            @pl.when(ck != c)
            def _():
                pltpu.make_async_copy(rowbuf.at[ck], rowbuf.at[ck], row_recv.at[ck]).wait()

            lanes = slice(k * bc, (k + 1) * bc)
            mask = keep_of(ck)
            for w in range(bw):
                abuf[32 * w:32 * w + 32, lanes] = spread(
                    rowbuf[ck, w:w + 1, :] & mask, 1.0).astype(jnp.bfloat16)
            for j in range(G):
                slot = j * C + ck

                @pl.when(slot != me)
                def _():
                    pltpu.make_async_copy(hubbuf.at[slot], hubbuf.at[slot], hub_recv.at[slot]).wait()

                for w in range(hw):
                    at = rows + 32 * (j * hw + w)
                    abuf[at:at + 32, lanes] = spread(
                        hubbuf[slot, w:w + 1, :] & mask, 1.0).astype(jnp.bfloat16)
        acc[...] += jnp.dot(abuf[...], bbuf[...], preferred_element_type=jnp.float32)
        return carry

    if R <= 4:
        for s in range(R):
            step(s, 0)
    else:
        lax.fori_loop(0, R, step, 0)

    for j in range(G):
        for w in range(hw):
            at = 32 * (j * hw + w)
            bbuf[at:at + 32, :pc] = spread(hubbuf[j * C + c, w:w + 1, part], 2.0).astype(jnp.bfloat16)
            for k in range(q):
                abuf[at:at + 32, k * bc:(k + 1) * bc] = spread(
                    hubbuf[j * C + r * q + k, w:w + 1, :], 1.0).astype(jnp.bfloat16)
    acc[:rows, :] += lax.dot_general(
        abuf[:nh, :], bbuf[:nh, :], (((0,), (0,)), ((), ())), preferred_element_type=jnp.float32)

    mask = jnp.concatenate(
        [keep[pl.ds(c * tiles + g * (pc // LANES) + t, 1), :] for t in range(pc // LANES)], axis=1)

    def close(row, at):
        hit = spread(row & mask, acc[at:at + 32, :pc])
        wsum[at:at + 32, :] = functools.reduce(
            jnp.add, [hit[:, t * LANES:(t + 1) * LANES] for t in range(pc // LANES)])

    for w in range(bw):
        close(rowbuf[c, w:w + 1, part], 32 * w)
    for j in range(G):
        for w in range(hw):
            close(hubbuf[j * C + c, w:w + 1, part], rows + 32 * (j * hw + w))

    hub_tri = jnp.sum(wsum[rows:, :], axis=1, keepdims=True)

    def partial(to):
        hits = hub_hits(r * rows + to * per)
        light = 1.0 - jnp.sum(jnp.where(hits, 1.0, 0.0), axis=0, keepdims=True)
        start = pl.multiple_of(to * per, 8)
        own_sum = jnp.sum(jnp.transpose(wsum[pl.ds(start, LANES), :]), axis=0, keepdims=True)
        return light * own_sum + jnp.sum(jnp.where(hits, hub_tri, 0.0), axis=0, keepdims=True)

    posts = []
    for d in range(1, G * C):
        slot, peer = group_peer(d)
        outbox[d] = partial(lax.rem(slot, C))
        post = pltpu.make_async_remote_copy(
            src_ref=outbox.at[d], dst_ref=inbox.at[me], send_sem=msg_send.at[d], recv_sem=msg_recv.at[me],
            device_id=peer, device_id_type=MESH)
        post.start()
        posts.append(post)

    tri = partial(c)
    hits = hub_hits(r * rows + c * per)
    light = 1.0 - jnp.sum(jnp.where(hits, 1.0, 0.0), axis=0, keepdims=True)
    start = pl.multiple_of(c * per, 8)
    deg = light * jnp.transpose(acc[pl.ds(start, LANES), pc:])[:1, :]
    deg = deg + jnp.sum(jnp.where(hits, acc[rows:, pc:], 0.0), axis=0, keepdims=True)
    for d in range(1, G * C):
        slot, _ = group_peer(d)
        pltpu.make_async_copy(inbox.at[slot], inbox.at[slot], msg_recv.at[slot]).wait()
        tri = tri + inbox[slot]
    out_ref[...] = (0.5 * tri / (1.0 + deg))[:, :per]
    for copy in sends + posts:
        copy.wait_send()


def body(light_bits, hub_bits, hub_ids):
    R, C, G = lax.axis_size("rows"), lax.axis_size("cols"), lax.axis_size("hub")
    bw, bc = light_bits.shape
    hw = hub_bits.shape[0]
    nh = hub_ids.shape[0]
    rows, pc = 32 * bw, bc // G
    per = rows // C
    dma = pltpu.SemaphoreType.DMA
    out = pl.pallas_call(
        functools.partial(kernel, R, C, G),
        out_shape=jax.ShapeDtypeStruct((1, per), jnp.float32),
        in_specs=[
            pl.BlockSpec(memory_space=pl.ANY),
            pl.BlockSpec(memory_space=pl.ANY),
            pl.BlockSpec(memory_space=pltpu.VMEM),
        ],
        out_specs=pl.BlockSpec(memory_space=pltpu.VMEM),
        scratch_shapes=[
            pltpu.VMEM((C, bw, bc), jnp.int32),
            pltpu.VMEM((R, bw, bc), jnp.int32),
            pltpu.VMEM((G * C, hw, bc), jnp.int32),
            pltpu.VMEM((C * bc // LANES, LANES), jnp.int32),
            pltpu.VMEM((nh, LANES), jnp.int32),
            pltpu.VMEM((rows + nh, rows), jnp.bfloat16),
            pltpu.VMEM((rows, pc + LANES), jnp.bfloat16),
            pltpu.VMEM((rows + nh, pc + LANES), jnp.float32),
            pltpu.VMEM((rows + nh, LANES), jnp.float32),
            pltpu.VMEM((G * C, 1, LANES), jnp.float32),
            pltpu.VMEM((G * C, 1, LANES), jnp.float32),
            dma((3,)), dma((C,)), dma((C,)), dma((R,)), dma((R,)),
            dma((G * C,)), dma((G * C,)), dma((G * C,)), dma((G * C,)),
        ],
        compiler_params=pltpu.CompilerParams(
            collective_id=0, has_side_effects=True, vmem_limit_bytes=56 * 1024 * 1024),
    )(light_bits, hub_bits, hub_ids.reshape(nh // LANES, LANES))
    return out.reshape(per)


def solution(mesh):
    return jax.shard_map(
        body,
        mesh=mesh,
        in_specs=(P("rows", "cols"), P("hub", "cols"), P()),
        out_specs=P(("rows", "cols")),
        check_vma=False,
    )
```

time: 143 us -> 25.2 us (0.18)
  blocking collectives: 130 us -> 0 us
  Pallas kernels: 0 us -> 23.9 us
  other arithmetic: 9.4 us -> 0 us
  matrix products: 2.72 us -> 0 us
    all_gather x3 -> x0, blocking collectives: 69.5 us -> none  [the longest x1 32.8 us: body(): hub_whole = lax.all_gather(hub_bits, 'cols', axis=1, tiled=True)]
    psum x2 -> x0, blocking collectives: 60.1 us -> none  [the longest x1 39.5 us: body(): lax.psum((hub_tri_full, hub_deg_full), ('rows', 'cols', 'hub'))]
    pallas_call x0 -> x1, Pallas kernels: none -> 23.9 us  [body(): pl.pallas_call(functools.partial(kernel, R, C, G), out_shape=jax.ShapeDty...]
    reduce_or x3 -> x0, other arithmetic: 2.99 us -> none  [light_flags(): is_hub = jnp.any(vertex_ids[:, None] == hub_ids[None, :], axis=1)]
    dot_general x2 -> x0, matrix products: 2.72 us -> none  [the longest x1 2.31 us: body(): jnp.dot(row_slice, column_bits, preferred_element_type=jnp.float32)]
    reduce_sum x4 -> x0, other arithmetic: 2.26 us -> none  [the longest x1 1.19 us: body(): light_deg = jnp.sum(own_part, axis=1)]
    mul x6 -> x0, other arithmetic: 2.11 us -> none  [the longest x1 0.94 us: body(): column_bits = unpack(section) * keep_mid[:, None]]
where the time goes in v1:
time: 25.2 us; the launch traced here: 25 us
  Pallas kernels  23.9 us (95%)
  local copies, waits for them, and re-layouts  1.1 us (4%)
    pallas_call x1, Pallas kernels, body(): pl.pallas_call(functools.partial(kernel, R, C, G), out_shape=jax.ShapeDty...  23.9 us
    unnamed x3, local copies, waits for them, and re-layouts  1.1 us

profile of v1, /device:TPU:0, one launch (start us, length us, event | category | flops | bytes accessed | tf_op | source)
XLA Modules:
  0.0 25.0 jit_solution(16646915139563150892)
XLA Ops:
  0.0 23.9 %shard_map.37 = f32[1,96]{1,0:T(1,128)} custom-call(s32[24,384]{1,0:T(8,128)} %light_hbm.1, s32[4,384]{1,0:T(4,128)} %hub_hbm.1, s32[1,128]{1,0:T(1,128)} %bitcast.2), custom_call_target="tpu_custom_call" | custom-call | tf_op jit(solution)/shard_map/pallas_call | solution.py:212
  23.9 0.0 copy-start
  23.9 0.6 %copy-done = f32[1,96]{1,0:T(1,128)S(1)} copy-done((f32[1,96]{1,0:T(1,128)S(1)}, f32[1,96]{1,0:T(1,128)}, u32[]{:S(2)}) %copy-start) | copy-done | bytes 408
  24.5 0.5 %copy.5 = f32[96]{0:T(128)} copy(f32[96]{0:T(128)S(1)} %bitcast.3) | data formatting | bytes 768
Async XLA Ops:
  23.9 0.6 %copy-start = (f32[1,96]{1,0:T(1,128)S(1)}, f32[1,96]{1,0:T(1,128)}, u32[]{:S(2)}) copy-start(f32[1,96]{1,0:T(1,128)} %shard_map.37) | copy-start | bytes 1156

commit v2 on v1

--- a/solution.py
+++ b/solution.py
@@ -28,6 +28,7 @@
     pc = bc // G
     q = C // R
     rows = 32 * bw
+    wq = bw // q
     nh = 32 * hw * G
     per = rows // C
     me = g * C + c
@@ -58,12 +59,12 @@
         copy.wait()
     pl.semaphore_wait(barrier, G * C - 1 + R - 1)
 
+    half = C // 2
     sends = []
-    for d in range(1, C):
-        to = lax.rem(c + d, C)
+    for d in range(half, 0, -1):
         sends.append(pltpu.make_async_remote_copy(
             src_ref=rowbuf.at[c], dst_ref=rowbuf.at[c], send_sem=row_send.at[d], recv_sem=row_recv.at[c],
-            device_id=(r, to, g), device_id_type=MESH))
+            device_id=(r, lax.rem(c + C - d, C), g), device_id_type=MESH))
     for d in range(1, R):
         sends.append(pltpu.make_async_remote_copy(
             src_ref=colbuf.at[r], dst_ref=colbuf.at[r], send_sem=col_send.at[d], recv_sem=col_recv.at[r],
@@ -93,65 +94,63 @@
     def keep_of(block):
         return jnp.concatenate([keep[pl.ds(block * tiles + t, 1), :] for t in range(tiles)], axis=1)
 
-    bbuf[:, pc:] = jnp.full((bbuf.shape[0], LANES), 1.0, jnp.bfloat16)
     part = pl.ds(pl.multiple_of(g * pc, LANES), pc)
-    acc[...] = jnp.zeros_like(acc)
-
-    def step(s, carry):
-        off = (s + 1) // 2 if isinstance(s, int) and s % 2 else None
-        if isinstance(s, int):
-            off = (s + 1) // 2 if s % 2 else R - s // 2
-        else:
-            off = lax.select(lax.rem(s, 2) == 1, (s + 1) // 2, R - s // 2)
-        rk = lax.rem(c // q + off, R)
-
-        @pl.when(rk != r)
-        def _():
-            pltpu.make_async_copy(colbuf.at[rk], colbuf.at[rk], col_recv.at[rk]).wait()
-
+    first = (g == 0).astype(jnp.float32)
+    ones = jnp.full((bc, LANES), 1.0, jnp.float32)
+
+    def load(d):
+        ck = lax.rem(c + d, C)
+        rk = ck // q
+        base = d * bc
+        weight = 1.0 if d == 0 or 2 * d == C else 2.0
+        word0 = lax.rem(ck, q) * wq
+        for w in range(wq):
+            at = base + 32 * w
+            bbuf[at:at + 32, :pc] = spread(colbuf[rk, pl.ds(word0 + w, 1), part], weight).astype(jnp.bfloat16)
+        bbuf[base:base + bc, pc:] = (ones * (first if d == 0 else 0.0)).astype(jnp.bfloat16)
+        mask = keep_of(ck)
         for w in range(bw):
-            bbuf[32 * w:32 * w + 32, :pc] = spread(colbuf[rk, w:w + 1, part], 1.0).astype(jnp.bfloat16)
-        for k in range(q):
-            ck = rk * q + k
-
-            @pl.when(ck != c)
-            def _():
-                pltpu.make_async_copy(rowbuf.at[ck], rowbuf.at[ck], row_recv.at[ck]).wait()
-
-            lanes = slice(k * bc, (k + 1) * bc)
-            mask = keep_of(ck)
-            for w in range(bw):
-                abuf[32 * w:32 * w + 32, lanes] = spread(
-                    rowbuf[ck, w:w + 1, :] & mask, 1.0).astype(jnp.bfloat16)
-            for j in range(G):
-                slot = j * C + ck
-
-                @pl.when(slot != me)
-                def _():
-                    pltpu.make_async_copy(hubbuf.at[slot], hubbuf.at[slot], hub_recv.at[slot]).wait()
-
-                for w in range(hw):
-                    at = rows + 32 * (j * hw + w)
-                    abuf[at:at + 32, lanes] = spread(
-                        hubbuf[slot, w:w + 1, :] & mask, 1.0).astype(jnp.bfloat16)
-        acc[...] += jnp.dot(abuf[...], bbuf[...], preferred_element_type=jnp.float32)
-        return carry
-
-    if R <= 4:
-        for s in range(R):
-            step(s, 0)
-    else:
-        lax.fori_loop(0, R, step, 0)
-
+            abuf[32 * w:32 * w + 32, base:base + bc] = spread(
+                rowbuf[ck, w:w + 1, :] & mask, 1.0).astype(jnp.bfloat16)
+        for j in range(G):
+            for w in range(hw):
+                at = rows + 32 * (j * hw + w)
+                abuf[at:at + 32, base:base + bc] = spread(
+                    hubbuf[j * C + ck, w:w + 1, :] & mask, 1.0).astype(jnp.bfloat16)
+
+    for d in range(1, R):
+        slot = col_peer(d)[0]
+        pltpu.make_async_copy(colbuf.at[slot], colbuf.at[slot], col_recv.at[slot]).wait()
+    load(0)
+    for d in range(1, G * C):
+        slot = group_peer(d)[0]
+        pltpu.make_async_copy(hubbuf.at[slot], hubbuf.at[slot], hub_recv.at[slot]).wait()
+
+    tail = (half + 1) * bc
+    once = first * (c == 0).astype(jnp.float32)
     for j in range(G):
         for w in range(hw):
-            at = 32 * (j * hw + w)
+            at = tail + 32 * (j * hw + w)
             bbuf[at:at + 32, :pc] = spread(hubbuf[j * C + c, w:w + 1, part], 2.0).astype(jnp.bfloat16)
-            for k in range(q):
-                abuf[at:at + 32, k * bc:(k + 1) * bc] = spread(
-                    hubbuf[j * C + r * q + k, w:w + 1, :], 1.0).astype(jnp.bfloat16)
-    acc[:rows, :] += lax.dot_general(
-        abuf[:nh, :], bbuf[:nh, :], (((0,), (0,)), ((), ())), preferred_element_type=jnp.float32)
+    bbuf[tail:, pc:] = jnp.broadcast_to(once, (nh, LANES)).astype(jnp.bfloat16)
+    abuf[rows:, tail:] = jnp.zeros((nh, nh), jnp.bfloat16)
+    for j in range(G):
+        for k in range(q):
+            bits = jnp.concatenate(
+                [spread(hubbuf[j * C + r * q + k, w:w + 1, :], 1.0) for w in range(hw)], axis=0)
+            lanes = slice(tail + 32 * hw * j, tail + 32 * hw * (j + 1))
+            abuf[k * bc:(k + 1) * bc, lanes] = jnp.transpose(bits).astype(jnp.bfloat16)
+
+    done = 0
+    for d in range(1, half + 1):
+        ck = lax.rem(c + d, C)
+        pltpu.make_async_copy(rowbuf.at[ck], rowbuf.at[ck], row_recv.at[ck]).wait()
+        load(d)
+        if d % 2 or d == half:
+            end = tail + nh if d == half else (d + 1) * bc
+            part_sum = jnp.dot(abuf[:, done:end], bbuf[done:end, :], preferred_element_type=jnp.float32)
+            acc[...] = part_sum if done == 0 else acc[...] + part_sum
+            done = end
 
     mask = jnp.concatenate(
         [keep[pl.ds(c * tiles + g * (pc // LANES) + t, 1), :] for t in range(pc // LANES)], axis=1)
@@ -176,10 +175,19 @@
         own_sum = jnp.sum(jnp.transpose(wsum[pl.ds(start, LANES), :]), axis=0, keepdims=True)
         return light * own_sum + jnp.sum(jnp.where(hits, hub_tri, 0.0), axis=0, keepdims=True)
 
+    def degrees(to):
+        hits = hub_hits(r * rows + to * per)
+        light = 1.0 - jnp.sum(jnp.where(hits, 1.0, 0.0), axis=0, keepdims=True)
+        start = pl.multiple_of(to * per, 8)
+        own_sum = jnp.transpose(acc[pl.ds(start, LANES), pc:])[:1, :]
+        return light * own_sum + jnp.sum(jnp.where(hits, acc[rows:, pc:], 0.0), axis=0, keepdims=True)
+
     posts = []
     for d in range(1, G * C):
         slot, peer = group_peer(d)
-        outbox[d] = partial(lax.rem(slot, C))
+        to = lax.rem(slot, C)
+        outbox[d, 0:1, :] = partial(to)
+        outbox[d, 1:2, :] = degrees(to)
         post = pltpu.make_async_remote_copy(
             src_ref=outbox.at[d], dst_ref=inbox.at[me], send_sem=msg_send.at[d], recv_sem=msg_recv.at[me],
             device_id=peer, device_id_type=MESH)
@@ -187,15 +195,12 @@
         posts.append(post)
 
     tri = partial(c)
-    hits = hub_hits(r * rows + c * per)
-    light = 1.0 - jnp.sum(jnp.where(hits, 1.0, 0.0), axis=0, keepdims=True)
-    start = pl.multiple_of(c * per, 8)
-    deg = light * jnp.transpose(acc[pl.ds(start, LANES), pc:])[:1, :]
-    deg = deg + jnp.sum(jnp.where(hits, acc[rows:, pc:], 0.0), axis=0, keepdims=True)
+    deg = degrees(c)
     for d in range(1, G * C):
         slot, _ = group_peer(d)
         pltpu.make_async_copy(inbox.at[slot], inbox.at[slot], msg_recv.at[slot]).wait()
-        tri = tri + inbox[slot]
+        tri = tri + inbox[slot, 0:1, :]
+        deg = deg + inbox[slot, 1:2, :]
     out_ref[...] = (0.5 * tri / (1.0 + deg))[:, :per]
     for copy in sends + posts:
         copy.wait_send()
@@ -208,6 +213,7 @@
     nh = hub_ids.shape[0]
     rows, pc = 32 * bw, bc // G
     per = rows // C
+    depth = (C // 2 + 1) * bc + nh
     dma = pltpu.SemaphoreType.DMA
     out = pl.pallas_call(
         functools.partial(kernel, R, C, G),
@@ -224,12 +230,12 @@
             pltpu.VMEM((G * C, hw, bc), jnp.int32),
             pltpu.VMEM((C * bc // LANES, LANES), jnp.int32),
             pltpu.VMEM((nh, LANES), jnp.int32),
-            pltpu.VMEM((rows + nh, rows), jnp.bfloat16),
-            pltpu.VMEM((rows, pc + LANES), jnp.bfloat16),
+            pltpu.VMEM((rows + nh, depth), jnp.bfloat16),
+            pltpu.VMEM((depth, pc + LANES), jnp.bfloat16),
             pltpu.VMEM((rows + nh, pc + LANES), jnp.float32),
             pltpu.VMEM((rows + nh, LANES), jnp.float32),
-            pltpu.VMEM((G * C, 1, LANES), jnp.float32),
-            pltpu.VMEM((G * C, 1, LANES), jnp.float32),
+            pltpu.VMEM((G * C, 2, LANES), jnp.float32),
+            pltpu.VMEM((G * C, 2, LANES), jnp.float32),
             dma((3,)), dma((C,)), dma((C,)), dma((R,)), dma((R,)),
             dma((G * C,)), dma((G * C,)), dma((G * C,)), dma((G * C,)),
         ],

time: 25.2 us -> 23.5 us (0.933)
  Pallas kernels: 23.9 us -> 22.2 us
    pallas_call x1, Pallas kernels: 23.9 us -> 22.2 us  [body(): pl.pallas_call(functools.partial(kernel, R, C, G), out_shape=jax.ShapeDty...]
where the time goes in v2:
time: 23.5 us; the launch traced here: 23.3 us
  Pallas kernels  22.2 us (94%)
  local copies, waits for them, and re-layouts  1.1 us (5%)
    pallas_call x1, Pallas kernels, body(): pl.pallas_call(functools.partial(kernel, R, C, G), out_shape=jax.ShapeDty...  22.2 us
    unnamed x3, local copies, waits for them, and re-layouts  1.1 us

profile of v2, /device:TPU:0, one launch (start us, length us, event | category | flops | bytes accessed | tf_op | source)
XLA Modules:
  0.0 23.3 jit_solution(17391937393498720980)
XLA Ops:
  0.0 22.2 %shard_map.37 = f32[1,96]{1,0:T(1,128)} custom-call(s32[24,384]{1,0:T(8,128)} %light_hbm.1, s32[4,384]{1,0:T(4,128)} %hub_hbm.1, s32[1,128]{1,0:T(1,128)} %bitcast.2), custom_call_target="tpu_custom_call" | custom-call | tf_op jit(solution)/shard_map/pallas_call | solution.py:218
  22.2 0.0 copy-start
  22.2 0.6 %copy-done = f32[1,96]{1,0:T(1,128)S(1)} copy-done((f32[1,96]{1,0:T(1,128)S(1)}, f32[1,96]{1,0:T(1,128)}, u32[]{:S(2)}) %copy-start) | copy-done | bytes 408
  22.8 0.5 %copy.5 = f32[96]{0:T(128)} copy(f32[96]{0:T(128)S(1)} %bitcast.3) | data formatting | bytes 768
Async XLA Ops:
  22.2 0.6 %copy-start = (f32[1,96]{1,0:T(1,128)S(1)}, f32[1,96]{1,0:T(1,128)}, u32[]{:S(2)}) copy-start(f32[1,96]{1,0:T(1,128)} %shard_map.37) | copy-start | bytes 1156

commit v3 on v2

--- a/solution.py
+++ b/solution.py
@@ -19,7 +19,7 @@
 def kernel(
     R, C, G,
     light_hbm, hub_hbm, ids_ref, out_ref,
-    rowbuf, colbuf, hubbuf, keep, hubcol, abuf, bbuf, acc, wsum, outbox, inbox,
+    rowbuf, colbuf, hubbuf, keep, hubcol, abuf, bbuf, acc, wsum, outbox, inbox, flags,
     local_sem, row_send, row_recv, col_send, col_recv, hub_send, hub_recv, msg_send, msg_recv,
 ):
     r, c, g = lax.axis_index("rows"), lax.axis_index("cols"), lax.axis_index("hub")
@@ -60,6 +60,25 @@
     pl.semaphore_wait(barrier, G * C - 1 + R - 1)
 
     half = C // 2
+    home = c // q == r
+    inner = jnp.logical_and(4 * c >= C, 4 * c < 3 * C)
+
+    def hub_copy(dj, d):
+        return pltpu.make_async_remote_copy(
+            src_ref=hubbuf.at[me], dst_ref=hubbuf.at[me], send_sem=hub_send.at[dj * C + d],
+            recv_sem=hub_recv.at[me], device_id_type=MESH,
+            device_id=(r, lax.rem(c + C - d, C), lax.rem(g + G - dj, G)))
+
+    hub_offsets = [(dj, d) for d in range(C - 1, -1, -1) for dj in range(G) if dj or d]
+
+    def hub_moves(act):
+        for dj, d in hub_offsets:
+            if d <= half:
+                act(dj, d)
+            else:
+                pl.when(home)(functools.partial(act, dj, d))
+
+    hub_moves(lambda dj, d: hub_copy(dj, d).start())
     sends = []
     for d in range(half, 0, -1):
         sends.append(pltpu.make_async_remote_copy(
@@ -69,11 +88,8 @@
         sends.append(pltpu.make_async_remote_copy(
             src_ref=colbuf.at[r], dst_ref=colbuf.at[r], send_sem=col_send.at[d], recv_sem=col_recv.at[r],
             device_id=col_peer(d)[1], device_id_type=MESH))
-    for d in range(1, G * C):
-        sends.append(pltpu.make_async_remote_copy(
-            src_ref=hubbuf.at[me], dst_ref=hubbuf.at[me], send_sem=hub_send.at[d], recv_sem=hub_recv.at[me],
-            device_id=group_peer(d)[1], device_id_type=MESH))
-    for copy in sends:
+    pl.when(jnp.logical_not(inner))(sends[0].start)
+    for copy in sends[1:]:
         copy.start()
 
     for h in range(nh // LANES):
@@ -101,13 +117,14 @@
     def load(d):
         ck = lax.rem(c + d, C)
         rk = ck // q
-        base = d * bc
-        weight = 1.0 if d == 0 or 2 * d == C else 2.0
+        base = d * bc + (nh if d else 0)
+        weight = 1.0 if d == 0 else 2.0
         word0 = lax.rem(ck, q) * wq
         for w in range(wq):
             at = base + 32 * w
             bbuf[at:at + 32, :pc] = spread(colbuf[rk, pl.ds(word0 + w, 1), part], weight).astype(jnp.bfloat16)
-        bbuf[base:base + bc, pc:] = (ones * (first if d == 0 else 0.0)).astype(jnp.bfloat16)
+        if d == 0:
+            bbuf[base:base + bc, pc:] = (ones * first).astype(jnp.bfloat16)
         mask = keep_of(ck)
         for w in range(bw):
             abuf[32 * w:32 * w + 32, base:base + bc] = spread(
@@ -122,35 +139,64 @@
         slot = col_peer(d)[0]
         pltpu.make_async_copy(colbuf.at[slot], colbuf.at[slot], col_recv.at[slot]).wait()
     load(0)
-    for d in range(1, G * C):
-        slot = group_peer(d)[0]
+
+    def hub_wait(slot):
         pltpu.make_async_copy(hubbuf.at[slot], hubbuf.at[slot], hub_recv.at[slot]).wait()
 
-    tail = (half + 1) * bc
+    for dj, d in hub_offsets:
+        ck = lax.rem(c + d, C)
+        wait = functools.partial(hub_wait, lax.rem(g + dj, G) * C + ck)
+        if d <= half:
+            wait()
+        else:
+            pl.when(ck // q == r)(wait)
+
     once = first * (c == 0).astype(jnp.float32)
     for j in range(G):
         for w in range(hw):
-            at = tail + 32 * (j * hw + w)
+            at = bc + 32 * (j * hw + w)
             bbuf[at:at + 32, :pc] = spread(hubbuf[j * C + c, w:w + 1, part], 2.0).astype(jnp.bfloat16)
-    bbuf[tail:, pc:] = jnp.broadcast_to(once, (nh, LANES)).astype(jnp.bfloat16)
-    abuf[rows:, tail:] = jnp.zeros((nh, nh), jnp.bfloat16)
+    bbuf[bc:bc + nh, pc:] = jnp.broadcast_to(once, (nh, LANES)).astype(jnp.bfloat16)
+    abuf[rows:, bc:bc + nh] = jnp.zeros((nh, nh), jnp.bfloat16)
     for j in range(G):
         for k in range(q):
             bits = jnp.concatenate(
                 [spread(hubbuf[j * C + r * q + k, w:w + 1, :], 1.0) for w in range(hw)], axis=0)
-            lanes = slice(tail + 32 * hw * j, tail + 32 * hw * (j + 1))
+            lanes = slice(bc + 32 * hw * j, bc + 32 * hw * (j + 1))
             abuf[k * bc:(k + 1) * bc, lanes] = jnp.transpose(bits).astype(jnp.bfloat16)
-
-    done = 0
-    for d in range(1, half + 1):
+    done = bc + nh
+    acc[...] = jnp.dot(abuf[:, :done], bbuf[:done, :], preferred_element_type=jnp.float32)
+
+    def settle(to, d):
+        hits = hub_hits(r * rows + to * per)
+        light = 1.0 - jnp.sum(jnp.where(hits, 1.0, 0.0), axis=0, keepdims=True)
+        start = pl.multiple_of(to * per, 8)
+        own_sum = jnp.transpose(acc[pl.ds(start, LANES), pc:])[:1, :]
+        outbox[d, 1:2, :] = light * own_sum + jnp.sum(
+            jnp.where(hits, acc[rows:, pc:], 0.0), axis=0, keepdims=True)
+        flags[d] = light
+
+    for d in range(G * C):
+        settle(lax.rem(group_peer(d)[0], C), d)
+
+    def meet(d):
         ck = lax.rem(c + d, C)
         pltpu.make_async_copy(rowbuf.at[ck], rowbuf.at[ck], row_recv.at[ck]).wait()
         load(d)
-        if d % 2 or d == half:
-            end = tail + nh if d == half else (d + 1) * bc
-            part_sum = jnp.dot(abuf[:, done:end], bbuf[done:end, :], preferred_element_type=jnp.float32)
-            acc[...] = part_sum if done == 0 else acc[...] + part_sum
-            done = end
+
+    def add(begin, end):
+        acc[:, :pc] += jnp.dot(abuf[:, begin:end], bbuf[begin:end, :pc], preferred_element_type=jnp.float32)
+
+    for d in range(1, half):
+        meet(d)
+        if d % 2 == 0 or d == half - 1:
+            add(done, (d + 1) * bc + nh)
+            done = (d + 1) * bc + nh
+
+    @pl.when(inner)
+    def _():
+        meet(half)
+        add(done, (half + 1) * bc + nh)
 
     mask = jnp.concatenate(
         [keep[pl.ds(c * tiles + g * (pc // LANES) + t, 1), :] for t in range(pc // LANES)], axis=1)
@@ -168,41 +214,33 @@
 
     hub_tri = jnp.sum(wsum[rows:, :], axis=1, keepdims=True)
 
-    def partial(to):
+    def partial(to, d):
         hits = hub_hits(r * rows + to * per)
-        light = 1.0 - jnp.sum(jnp.where(hits, 1.0, 0.0), axis=0, keepdims=True)
         start = pl.multiple_of(to * per, 8)
         own_sum = jnp.sum(jnp.transpose(wsum[pl.ds(start, LANES), :]), axis=0, keepdims=True)
-        return light * own_sum + jnp.sum(jnp.where(hits, hub_tri, 0.0), axis=0, keepdims=True)
-
-    def degrees(to):
-        hits = hub_hits(r * rows + to * per)
-        light = 1.0 - jnp.sum(jnp.where(hits, 1.0, 0.0), axis=0, keepdims=True)
-        start = pl.multiple_of(to * per, 8)
-        own_sum = jnp.transpose(acc[pl.ds(start, LANES), pc:])[:1, :]
-        return light * own_sum + jnp.sum(jnp.where(hits, acc[rows:, pc:], 0.0), axis=0, keepdims=True)
+        return flags[d] * own_sum + jnp.sum(jnp.where(hits, hub_tri, 0.0), axis=0, keepdims=True)
 
     posts = []
-    for d in range(1, G * C):
+    for d in sorted(range(1, G * C), key=lambda d: abs(2 * d - G * C)):
         slot, peer = group_peer(d)
-        to = lax.rem(slot, C)
-        outbox[d, 0:1, :] = partial(to)
-        outbox[d, 1:2, :] = degrees(to)
+        outbox[d, 0:1, :] = partial(lax.rem(slot, C), d)
         post = pltpu.make_async_remote_copy(
             src_ref=outbox.at[d], dst_ref=inbox.at[me], send_sem=msg_send.at[d], recv_sem=msg_recv.at[me],
             device_id=peer, device_id_type=MESH)
         post.start()
         posts.append(post)
 
-    tri = partial(c)
-    deg = degrees(c)
+    tri = partial(c, 0)
+    deg = outbox[0, 1:2, :]
     for d in range(1, G * C):
         slot, _ = group_peer(d)
         pltpu.make_async_copy(inbox.at[slot], inbox.at[slot], msg_recv.at[slot]).wait()
         tri = tri + inbox[slot, 0:1, :]
         deg = deg + inbox[slot, 1:2, :]
     out_ref[...] = (0.5 * tri / (1.0 + deg))[:, :per]
-    for copy in sends + posts:
+    hub_moves(lambda dj, d: hub_copy(dj, d).wait_send())
+    pl.when(jnp.logical_not(inner))(sends[0].wait_send)
+    for copy in sends[1:] + posts:
         copy.wait_send()
 
 
@@ -236,6 +274,7 @@
             pltpu.VMEM((rows + nh, LANES), jnp.float32),
             pltpu.VMEM((G * C, 2, LANES), jnp.float32),
             pltpu.VMEM((G * C, 2, LANES), jnp.float32),
+            pltpu.VMEM((G * C, 1, LANES), jnp.float32),
             dma((3,)), dma((C,)), dma((C,)), dma((R,)), dma((R,)),
             dma((G * C,)), dma((G * C,)), dma((G * C,)), dma((G * C,)),
         ],

time: 23.5 us -> 22.2 us (0.945)
  Pallas kernels: 22.2 us -> 20.9 us
    pallas_call x1, Pallas kernels: 22.2 us -> 20.9 us  [body(): pl.pallas_call(functools.partial(kernel, R, C, G), out_shape=jax.ShapeDty...]
where the time goes in v3:
time: 22.2 us; the launch traced here: 22 us
  Pallas kernels  20.9 us (94%)
  local copies, waits for them, and re-layouts  1.1 us (5%)
    pallas_call x1, Pallas kernels, body(): pl.pallas_call(functools.partial(kernel, R, C, G), out_shape=jax.ShapeDty...  20.9 us
    unnamed x3, local copies, waits for them, and re-layouts  1.1 us

profile of v3, /device:TPU:0, one launch (start us, length us, event | category | flops | bytes accessed | tf_op | source)
XLA Modules:
  0.0 22.0 jit_solution(1432050032220660626)
XLA Ops:
  0.0 20.9 %shard_map.37 = f32[1,96]{1,0:T(1,128)} custom-call(s32[24,384]{1,0:T(8,128)} %light_hbm.1, s32[4,384]{1,0:T(4,128)} %hub_hbm.1, s32[1,128]{1,0:T(1,128)} %bitcast.2), custom_call_target="tpu_custom_call" | custom-call | tf_op jit(solution)/shard_map/pallas_call | solution.py:256
  20.9 0.0 copy-start
  20.9 0.6 %copy-done = f32[1,96]{1,0:T(1,128)S(1)} copy-done((f32[1,96]{1,0:T(1,128)S(1)}, f32[1,96]{1,0:T(1,128)}, u32[]{:S(2)}) %copy-start) | copy-done | bytes 408
  21.5 0.5 %copy.5 = f32[96]{0:T(128)} copy(f32[96]{0:T(128)S(1)} %bitcast.3) | data formatting | bytes 768
Async XLA Ops:
  20.9 0.6 %copy-start = (f32[1,96]{1,0:T(1,128)S(1)}, f32[1,96]{1,0:T(1,128)}, u32[]{:S(2)}) copy-start(f32[1,96]{1,0:T(1,128)} %shard_map.37) | copy-start | bytes 1156
